TPU v7x, 256 devices: a whole 4x4x8 slice. The times are simulated.
256 devices in a mesh: expert: 8 (over y, core), shard: 32 (over x, z).
Axes of the slice: x: 4, y: 4, z: 8, core: 2. Of those that a mesh axis runs over, the one named last changes fastest.
Arguments:
- params: float32 [3, 8, 6144, 256], P(None, 'expert', 'shard'), may hold values from -3 to 3
- grads: float32 [3, 8, 6144, 256], P(None, 'expert', 'shard')
- moment: float32 [3, 8, 6144, 256], P(None, 'expert', 'shard'), may hold values from -0.6 to 0.6
- second: float32 [3, 8, 64], P(None, 'expert'), may hold values from 0.002 to 0.2
- step: int32 [1], replicated, may hold values from 1 to 8
- block_map: int32 [256], replicated, may hold values from 0 to 63, never falling along the last dimension, each value on 1 to 8 neighbouring positions
Outputs:
- new_weights: bfloat16 [3, 8, 6144, 256], P(None, 'expert')
- new_moment: float32 [3, 8, 6144, 256], P(None, 'expert', 'shard')
- new_second: float32 [3, 8, 64], P(None, 'expert')
Inputs may be any that keep to these rules, and one draw needn't show every extreme that they name: `block_map`: every block holds at least one neuron and at most 8.
All inputs are finite; a program needn't handle non-finite values.
Results may differ from a plain program's by a relative error of at most 0.001.
Values may be sent and summed in bfloat16 or wider, within the bound.
No kernel may reach another device: no remote copies, remote signals or barrier semaphores. Data moves between devices by JAX's collectives and lax.ppermute only.
A program may use at most 64 MiB of HBM per device.

v0:
```python
import math
import jax
import jax.numpy as jnp
from jax import lax
from jax.sharding import PartitionSpec as P

LEARN_RATE = 0.05
DECAY_WEIGHT = 0.1
BETA_FIRST = 0.9
BETA_SECOND = 0.95
epsilon = 1e-08


def copy_for_each(x, axis):
    length = lax.axis_size(axis)
    return lax.all_to_all(jnp.broadcast_to(x[None], (length, *x.shape)), axis, 0, 0, tiled=True)


def taken_together(x, axis):
    everything = copy_for_each(x, axis)
    return jnp.sum(everything, axis=0)


def body(params, grads, moment, second, step, block_map):
    blocks = second.shape[2]
    member_table = (block_map[:, None] == jnp.arange(blocks, dtype=jnp.int32)[None, :]).astype(
        jnp.float32
    )
    members = jnp.sum(member_table, axis=0)
    width = grads.shape[2] * lax.axis_size("shard")
    squares = jnp.sum(grads * grads, axis=2)
    local_sums = jnp.einsum("ken,nb->keb", squares, member_table, precision=lax.Precision.HIGHEST)
    block_sums = taken_together(local_sums, "shard")
    total = taken_together(jnp.sum(block_sums), "expert")
    limit = math.sqrt(3 * lax.axis_size("expert") * grads.shape[1] * width * grads.shape[3])
    clip = jnp.minimum(1.0, limit / (jnp.sqrt(total) + 1e-06))
    new_second = BETA_SECOND * second + (1.0 - BETA_SECOND) * clip * clip * block_sums / (
        width * members
    )
    new_moment = BETA_FIRST * moment + (1.0 - BETA_FIRST) * clip * grads
    step_value = step[0].astype(jnp.float32)
    first_fix = 1.0 - jnp.power(jnp.float32(BETA_FIRST), step_value)
    second_fix = 1.0 - jnp.power(jnp.float32(BETA_SECOND), step_value)
    divisor = jnp.sqrt(new_second / second_fix) + epsilon
    by_neuron = jnp.einsum("keb,nb->ken", divisor, member_table, precision=lax.Precision.HIGHEST)
    updated = (
        params * (1.0 - LEARN_RATE * DECAY_WEIGHT)
        - LEARN_RATE * (new_moment / first_fix) / by_neuron[:, :, None, :]
    )
    new_weights = lax.all_gather(updated.astype(jnp.bfloat16), "shard", axis=2, tiled=True)
    return (new_weights, new_moment, new_second)


def solution(mesh):
    placed = (
        P(None, "expert", "shard", None),
        P(None, "expert", "shard", None),
        P(None, "expert", "shard", None),
        P(None, "expert", None),
        P(),
        P(),
    )
    return jax.shard_map(
        body,
        mesh=mesh,
        in_specs=placed,
        out_specs=(
            P(None, "expert", None, None),
            P(None, "expert", "shard", None),
            P(None, "expert", None),
        ),
        check_vma=False,
    )
```

profile of v0, /device:TPU:1, one launch (start us, length us, event | category | flops | bytes accessed | tf_op | source)
XLA Modules:
  0.0 160.5 jit_solution(13806636719966661453)
XLA Ops:
  7.2 1.1 multiply_reduce_fusion
  8.3 0.8 fusion.1
  9.1 0.1 broadcast_in_dim.4
  9.2 0.5 broadcast.38
  9.7 0.8 reduce.4
  10.5 0.7 reshape.75
  11.2 11.9 %all-to-all-start = ((f32[32,1,192]{2,1,0:T(1,128)}), f32[32,1,192]{2,1,0:T(1,128)S(1)}, u32[]{:S(2)}, u32[]{:S(2)}) async-start(f32[32,1,192]{2,1,0:T(1,128)} %reshape.75), calls=%async_computation | async-start | bytes 65536 | tf_op jit(solution)/shard_map/all_to_all | solution.py:16
  23.0 0.0 all-gather.2.cloned.1.call-start
  23.1 0.8 convert_reduce_fusion
  24.6 7.2 %all-to-all-done = f32[32,1,192]{2,1,0:T(1,128)S(1)} async-done(((f32[32,1,192]{2,1,0:T(1,128)}), f32[32,1,192]{2,1,0:T(1,128)S(1)}, u32[]{:S(2)}, u32[]{:S(2)}) %all-to-all-start) | async-done | bytes 24608 | tf_op jit(solution)/shard_map/all_to_all | solution.py:16
  31.8 0.7 reduce.5
  32.5 0.1 reshape.76
  32.6 0.7 fusion.11
  33.3 0.6 broadcast_in_dim.5
  34.0 11.0 %all_to_all.11 = f32[8,1,1]{2,1,0:T(1,128)S(1)} all-to-all(f32[8,1,1]{2,1,0:T(1,128)S(1)} %broadcast_in_dim.5), channel_id=1, replica_groups=mesh['expert'=8,'shard'=32] {'expert'}, dimensions={0} | all-to-all | bytes 64 | tf_op jit(solution)/shard_map/all_to_all | solution.py:16
  45.0 0.6 reduce_sum.47
  46.3 0.7 divide_add_fusion
  47.0 0.8 fusion
  47.8 2.5 %subtract_convert_fusion = (bf16[3,1,192,256]{3,2,1,0:T(8,128)(2,1)}, f32[3,1,192,256]{3,2,1,0:T(8,128)}) fusion(f32[3,1,192,256]{3,2,1,0:T(8,128)} %param.6, f32[3,256]{1,0:T(4,128)S(1)} %fusion, f32[]{:T(128)} %bitcast, f32[3,1,192,256]{3,2,1,0:T(8,128)} %param.7, f32[]{:T(128)S(6)} %mul_shard_map.3, f32[3,1,192,256]{3,2,1,0:T(8,128)} %param.8), kind=kLoop, calls=%fused_computation | loop fusion | flops 1327104 | bytes 2657288 | tf_op jit(solution)/shard_map/convert_element_type | solution.py:50
  50.3 0.0 all-gather.2.cloned.1.call-update
  50.3 0.6 copy.15
  50.9 94.7 %all-gather.2.cloned.1.call-done = bf16[3,1,6144,256]{3,2,1,0:T(8,128)(2,1)} async-done(((bf16[3,1,192,256]{3,2,1,0:T(8,128)(2,1)}), bf16[3,1,6144,256]{3,2,1,0:T(8,128)(2,1)}) %all-gather.2.cloned.1.call-update) | async-done | bytes 9437200 | tf_op jit(solution)/shard_map/all_gather | solution.py:50
  145.6 8.0 %copy.24 = bf16[3,1,6144,256]{3,2,1,0:T(8,128)(2,1)} copy(bf16[3,1,6144,256]{3,2,1,0:T(8,128)(2,1)} %all-gather.2.cloned.1.call-done) | data formatting | bytes 18874368
  (1 shorter events, 0.0 us)
Async XLA Ops:
  11.2 20.6 %all-to-all-start = ((f32[32,1,192]{2,1,0:T(1,128)}), f32[32,1,192]{2,1,0:T(1,128)S(1)}, u32[]{:S(2)}, u32[]{:S(2)}) async-start(f32[32,1,192]{2,1,0:T(1,128)} %reshape.75), calls=%async_computation | async-start | bytes 65536 | tf_op jit(solution)/shard_map/all_to_all | solution.py:16
  23.0 122.6 %all-gather.2.cloned.1.call-start = ((), (), s32[]{:S(2)}) async-start(), calls=%async_computation.2 | async-start | bytes 9732096 | tf_op jit(solution)/shard_map/all_gather | solution.py:50
Sparse Core Ops, SparseCore 0:
  50.5 95.1 all-gather.1
where the time goes:
time: 161 us; the launch traced here: 160 us
  waiting for transfers between devices  102 us (63%)
  between operations  15.6 us (10%)
  starting transfers between devices  11.9 us (7%)
  blocking collectives  11 us (7%)
  local copies, waits for them, and re-layouts  10.6 us (7%)
  other arithmetic  7.94 us (5%)
  matrix products  1.61 us (1%)
    all_gather x1, waiting for transfers between devices, body(): lax.all_gather(updated.astype(jnp.bfloat16), 'shard', axis=2, tiled=True)  94.7 us
    all_to_all x1, starting transfers between devices, copy_for_each(): lax.all_to_all(jnp.broadcast_to(x[None], (length, *x.shape)), axis, 0, 0,...  11.9 us
    all_to_all x1, blocking collectives, copy_for_each(): lax.all_to_all(jnp.broadcast_to(x[None], (length, *x.shape)), axis, 0, 0,...  11 us
    unnamed x4, local copies, waits for them, and re-layouts  9.39 us
    all_to_all x1, waiting for transfers between devices, copy_for_each(): lax.all_to_all(jnp.broadcast_to(x[None], (length, *x.shape)), axis, 0, 0,...  7.18 us
  transfers between devices with their start and end apart: 2, of which 2 were waited for; matrix products, arithmetic and copies ran while one was open for 1% of the time, Pallas kernels for 0%

commit v1 on v0

--- a/solution.py
+++ b/solution.py
@@ -9,6 +9,11 @@
 BETA_FIRST = 0.9
 BETA_SECOND = 0.95
 epsilon = 1e-08
+
+
+def gather_by_exchange(x, axis, dim):
+    copies = jnp.concatenate([x] * lax.axis_size(axis), axis=dim)
+    return lax.all_to_all(copies, axis, dim, dim, tiled=True)
 
 
 def copy_for_each(x, axis):
@@ -47,7 +52,7 @@
         params * (1.0 - LEARN_RATE * DECAY_WEIGHT)
         - LEARN_RATE * (new_moment / first_fix) / by_neuron[:, :, None, :]
     )
-    new_weights = lax.all_gather(updated.astype(jnp.bfloat16), "shard", axis=2, tiled=True)
+    new_weights = gather_by_exchange(updated.astype(jnp.bfloat16), "shard", 2)
     return (new_weights, new_moment, new_second)
 
 

time: 161 us -> 409 us (2.54)
  the two profiles are of different devices: /device:TPU:1 before, /device:TPU:167 now
where the time goes in v1:
time: 409 us
  waiting for transfers between devices  305 us (75%)
  local copies, waits for them, and re-layouts  62.4 us (15%)
  starting transfers between devices  19.3 us (5%)
  blocking collectives  10.7 us (3%)
  other arithmetic  7.84 us (2%)
    all_to_all x1, waiting for transfers between devices, gather_by_exchange(): return lax.all_to_all(copies, axis, dim, dim, tiled=True)  303 us
    concatenate x2, local copies, waits for them, and re-layouts, gather_by_exchange(): copies = jnp.concatenate([x] * lax.axis_size(axis), axis=dim)  49.5 us
    unnamed x34, local copies, waits for them, and re-layouts  11.6 us
    all_to_all x1, blocking collectives, copy_for_each(): lax.all_to_all(jnp.broadcast_to(x[None], (length, *x.shape)), axis, 0, 0,...  10.7 us
    all_to_all x1, starting transfers between devices, gather_by_exchange(): return lax.all_to_all(copies, axis, dim, dim, tiled=True)  10.5 us
    all_to_all x1, starting transfers between devices, copy_for_each(): lax.all_to_all(jnp.broadcast_to(x[None], (length, *x.shape)), axis, 0, 0,...  8.8 us
  transfers between devices with their start and end apart: 2, of which 2 were waited for; matrix products, arithmetic and copies ran while one was open for 0% of the time, Pallas kernels for 0%

profile of v1, /device:TPU:167, one launch (start us, length us, event | category | flops | bytes accessed | tf_op | source)
XLA Modules:
  0.0 408.8 jit_solution(12837783588795937898)
XLA Ops:
  0.6 1.1 multiply_reduce_fusion
  1.8 0.8 fusion.1
  2.6 0.1 broadcast_in_dim.4
  2.6 0.5 broadcast.38
  3.1 0.8 reduce.4
  3.9 0.7 reshape.75
  4.6 8.8 %all-to-all-start = ((f32[32,1,192]{2,1,0:T(1,128)}), f32[32,1,192]{2,1,0:T(1,128)S(1)}, u32[]{:S(2)}, u32[]{:S(2)}) async-start(f32[32,1,192]{2,1,0:T(1,128)} %reshape.75), calls=%async_computation | async-start | bytes 65536 | tf_op jit(solution)/shard_map/all_to_all | solution.py:21
  13.4 0.8 convert_reduce_fusion
  15.0 2.0 all-to-all-done
  17.0 0.7 reduce.5
  17.7 0.1 reshape.76
  17.8 0.7 fusion.11
  18.5 0.6 broadcast_in_dim.5
  19.1 10.7 %all_to_all.16 = f32[8,1,1]{2,1,0:T(1,128)S(1)} all-to-all(f32[8,1,1]{2,1,0:T(1,128)S(1)} %broadcast_in_dim.5), channel_id=1, replica_groups=mesh['expert'=8,'shard'=32] {'expert'}, dimensions={0} | all-to-all | bytes 64 | tf_op jit(solution)/shard_map/all_to_all | solution.py:21
  29.9 0.6 reduce_sum.47
  31.2 0.7 divide_add_fusion
  31.9 0.8 fusion
  32.7 2.4 constant_dynamic-update-slice_fusion.31
  36.0 49.5 %copy.27 = bf16[3,1,6144,256]{3,0,1,2:T(4,128)(2,1)} copy(bf16[3,1,6144,256]{3,2,1,0:T(8,128)(2,1)S(1)} %constant_dynamic-update-slice_fusion) | data formatting | bytes 18874368 | tf_op jit(solution)/shard_map/concatenate | solution.py:15
  85.5 10.5 %all-to-all-start.2 = ((bf16[3,1,6144,256]{3,0,1,2:T(4,128)(2,1)}), bf16[3,1,6144,256]{3,0,1,2:T(4,128)(2,1)}, u32[]{:S(2)}, u32[]{:S(2)}) async-start(bf16[3,1,6144,256]{3,0,1,2:T(4,128)(2,1)} %copy.27), calls=%async_computation.2 | async-start | bytes 25165824 | tf_op jit(solution)/shard_map/all_to_all | solution.py:16
  96.0 0.6 copy.29
  96.6 302.6 %all-to-all-done.2 = bf16[3,1,6144,256]{3,0,1,2:T(4,128)(2,1)} async-done(((bf16[3,1,6144,256]{3,0,1,2:T(4,128)(2,1)}), bf16[3,1,6144,256]{3,0,1,2:T(4,128)(2,1)}, u32[]{:S(2)}, u32[]{:S(2)}) %all-to-all-start.2) | async-done | bytes 9437216 | tf_op jit(solution)/shard_map/all_to_all | solution.py:16
  399.1 9.6 %copy.28 = bf16[3,1,6144,256]{3,2,1,0:T(8,128)(2,1)} copy(bf16[3,1,6144,256]{3,0,1,2:T(4,128)(2,1)} %all-to-all-done.2) | data formatting | bytes 18874368
  (32 shorter events, 0.7 us)
Async XLA Ops:
  4.6 12.3 %all-to-all-start = ((f32[32,1,192]{2,1,0:T(1,128)}), f32[32,1,192]{2,1,0:T(1,128)S(1)}, u32[]{:S(2)}, u32[]{:S(2)}) async-start(f32[32,1,192]{2,1,0:T(1,128)} %reshape.75), calls=%async_computation | async-start | bytes 65536 | tf_op jit(solution)/shard_map/all_to_all | solution.py:21
  85.5 313.6 %all-to-all-start.2 = ((bf16[3,1,6144,256]{3,0,1,2:T(4,128)(2,1)}), bf16[3,1,6144,256]{3,0,1,2:T(4,128)(2,1)}, u32[]{:S(2)}, u32[]{:S(2)}) async-start(bf16[3,1,6144,256]{3,0,1,2:T(4,128)(2,1)} %copy.27), calls=%async_computation.2 | async-start | bytes 25165824 | tf_op jit(solution)/shard_map/all_to_all | solution.py:16
